TPU v7x, 256 devices: a whole 4x4x8 slice. The times are simulated.
256 devices in a mesh: row: 8 (over z), col: 16 (over y_lo, x, core), layer: 2 (over y_hi).
Axes of the slice: x: 4, y: 4 (y_hi: 2, y_lo: 2; y = y_hi * 2 + y_lo), z: 8, core: 2. Of those that a mesh axis runs over, the one named last changes fastest.
Arguments:
- left: bfloat16 [8192, 8192], P('row', ('col', 'layer')), may hold values from -6 to 6
- middle: bfloat16 [8192, 8192], P('row', 'col'), may hold values from -0.0625 to 0.0625
- right: bfloat16 [8192, 8192], P('row', 'col'), may hold values from -0.0625 to 0.0625
Outputs:
- product: bfloat16 [8192, 8192], P('row', ('col', 'layer'))
All inputs are finite; a program needn't handle non-finite values.
Results may differ from a plain program's by a relative error of at most 0.0049.
Values may be sent and summed in bfloat16 or wider, within the bound.
A program may use at most 64 MiB of HBM per device.

v0:
```python
import jax
import jax.numpy as jnp
from jax import lax
from jax.sharding import PartitionSpec as P


def split_up(array, dim, size):
    lengths = array.shape
    blocks = array.reshape(*lengths[:dim], size, lengths[dim] // size, *lengths[dim + 1 :])
    return jnp.moveaxis(blocks, dim, 0)


def sum_at_owner(array, axis, dim):
    blocks = split_up(array, dim, lax.axis_size(axis))
    arrived = lax.all_to_all(blocks, axis, split_axis=0, concat_axis=0, tiled=True)
    return arrived.sum(axis=0)


def multiply(left, right):
    width = left.shape[1]
    layers = lax.axis_size("layer")
    layer_index = lax.axis_index("layer")
    columns = right.shape[1]
    groups = right.shape[0] // width // layers
    shaped = right.reshape(groups, layers, width, columns)
    own_rows = lax.dynamic_index_in_dim(shaped, layer_index, 1, keepdims=False).reshape(
        groups * width, columns
    )
    right_all = lax.all_gather(own_rows, "row", axis=0, tiled=True)
    return jnp.dot(
        lax.all_gather(left, "col", axis=1, tiled=True),
        right_all,
        preferred_element_type=jnp.float32,
    )


def per_device(left, middle, right):
    partial_value = multiply(left, middle)
    first = sum_at_owner(partial_value, "layer", 1)
    first = first.astype(jnp.bfloat16)
    second = multiply(first, right)
    return sum_at_owner(second, "layer", 1).astype(jnp.bfloat16)


def solution(mesh):
    return jax.shard_map(
        per_device,
        mesh=mesh,
        in_specs=(P("row", ("col", "layer")), P("row", "col"), P("row", "col")),
        out_specs=P("row", ("col", "layer")),
        check_vma=False,
    )
```

profile of v0, /device:TPU:1, one launch (start us, length us, event | category | flops | bytes accessed | tf_op | source)
XLA Modules:
  0.0 290.7 jit_solution(16866077000397679622)
XLA Ops:
  6.5 0.0 copy-start
  6.5 0.0 all-gather.5.cloned.1.call-start
  6.5 1.2 copy-done
  7.8 0.8 constant_dynamic-slice_fusion.1
  8.6 0.0 all-gather.5.cloned.1.call-update
  8.6 0.0 all-gather.7.cloned.1.call-start
  8.7 0.7 all-gather.7.cloned.1.call-update
  9.4 0.0 all-gather.11.cloned.1.call-start
  9.4 1.9 constant_dynamic-slice_fusion
  11.3 0.0 all-gather.11.cloned.1.call-update
  11.3 0.0 all-gather.9.cloned.1.call-start
  11.4 56.2 %all-gather.5.cloned.1.call-done = bf16[4096,512]{1,0:T(8,128)(2,1)} async-done(((bf16[512,512]{1,0:T(8,128)(2,1)}), bf16[4096,512]{1,0:T(8,128)(2,1)}) %all-gather.5.cloned.1.call-update) | async-done | bytes 4194320 | tf_op jit(solution)/shard_map/all_gather | solution.py:29
  67.5 64.4 %all-gather.7.cloned.1.call-done = bf16[1024,4096]{1,0:T(8,128)(2,1)} async-done(((bf16[1024,256]{1,0:T(8,128)(2,1)}), bf16[1024,4096]{1,0:T(8,128)(2,1)}) %all-gather.7.cloned.1.call-update) | async-done | bytes 8388624 | tf_op jit(solution)/shard_map/all_gather | solution.py:31
  131.9 8.2 %fusion = f32[512,1024]{1,0:T(8,128)S(1)} fusion(bf16[4096,512]{1,0:T(8,128)(2,1)} %all-gather.5.cloned.1.call-done, bf16[1024,4096]{1,0:T(8,128)(2,1)} %all-gather.7.cloned.1.call-done), kind=kOutput, calls=%fused_computation.2 | convolution fusion | flops 4294967296 | bytes 14680064 | tf_op jit(solution)/shard_map/dot_general | solution.py:30
  140.1 28.8 %all_to_all.10 = f32[2,1024,256]{1,2,0:T(8,128)S(1)} all-to-all(f32[2,1024,256]{1,2,0:T(8,128)S(1)} %bitcast.17), channel_id=1, replica_groups=mesh['row'=8,'col'=16,'layer'=2] {'layer'}, dimensions={0} | all-to-all | bytes 4194304 | tf_op jit(solution)/shard_map/all_to_all | solution.py:15
  168.9 1.1 reduce_sum.18
  170.0 0.0 all-gather.9.cloned.1.call-update
  170.0 17.7 %all-gather.11.cloned.1.call-done = bf16[4096,512]{1,0:T(8,128)(2,1)} async-done(((bf16[512,512]{1,0:T(8,128)(2,1)}), bf16[4096,512]{1,0:T(8,128)(2,1)}) %all-gather.11.cloned.1.call-update) | async-done | bytes 4194320 | tf_op jit(solution)/shard_map/all_gather | solution.py:29
  187.7 55.5 %all-gather.9.cloned.1.call-done = bf16[1024,4096]{0,1:T(8,128)(2,1)} async-done(((bf16[1024,256]{0,1:T(8,128)(2,1)}), bf16[1024,4096]{0,1:T(8,128)(2,1)}) %all-gather.9.cloned.1.call-update) | async-done | bytes 8388624 | tf_op jit(solution)/shard_map/all_gather | solution.py:31
  243.2 8.2 %fusion.1 = f32[1024,512]{0,1:T(8,128)S(1)} fusion(bf16[1024,4096]{0,1:T(8,128)(2,1)} %all-gather.9.cloned.1.call-done, bf16[4096,512]{1,0:T(8,128)(2,1)} %all-gather.11.cloned.1.call-done), kind=kOutput, calls=%fused_computation.3 | convolution fusion | flops 4294967296 | bytes 14680064 | tf_op jit(solution)/shard_map/dot_general | solution.py:30
  251.4 29.6 %all_to_all.11 = f32[2,1024,256]{1,2,0:T(8,128)S(1)} all-to-all(f32[2,1024,256]{1,2,0:T(8,128)S(1)} %bitcast.18), channel_id=1, replica_groups=mesh['row'=8,'col'=16,'layer'=2] {'layer'}, dimensions={0} | all-to-all | bytes 4194304 | tf_op jit(solution)/shard_map/all_to_all | solution.py:15
  281.0 1.1 reduce_sum.19
  282.1 2.0 copy.4
Async XLA Ops:
  6.5 1.2 copy-start
  6.5 61.0 %all-gather.5.cloned.1.call-start = ((), (), s32[]{:S(2)}) async-start(), calls=%async_computation.2 | async-start | bytes 4718592 | tf_op jit(solution)/shard_map/all_gather | solution.py:29
  8.6 123.3 %all-gather.7.cloned.1.call-start = ((), (), s32[]{:S(2)}) async-start(), calls=%async_computation.3 | async-start | bytes 8912896 | tf_op jit(solution)/shard_map/all_gather | solution.py:31
  9.4 178.3 %all-gather.11.cloned.1.call-start = ((), (), s32[]{:S(2)}) async-start(), calls=%async_computation.5 | async-start | bytes 4718592 | tf_op jit(solution)/shard_map/all_gather | solution.py:29
  11.3 231.9 %all-gather.9.cloned.1.call-start = ((), (), s32[]{:S(2)}) async-start(), calls=%async_computation.4 | async-start | bytes 8912896 | tf_op jit(solution)/shard_map/all_gather | solution.py:31
Sparse Core Ops, SparseCore 0:
  9.1 58.3 all-gather.4
  69.3 62.5 all-gather.6
  133.7 53.9 all-gather.10
  189.4 53.7 all-gather.8
where the time goes:
time: 291 us
  waiting for transfers between devices  194 us (67%)
  blocking collectives  58.3 us (20%)
  matrix products  16.5 us (6%)
  between operations  13.1 us (5%)
  local copies, waits for them, and re-layouts  5.97 us (2%)
    all_gather x2, waiting for transfers between devices, multiply(): lax.all_gather(left, 'col', axis=1, tiled=True)  120 us
    all_gather x2, waiting for transfers between devices, multiply(): right_all = lax.all_gather(own_rows, 'row', axis=0, tiled=True)  73.8 us
    all_to_all x2, blocking collectives, sum_at_owner(): lax.all_to_all(blocks, axis, split_axis=0, concat_axis=0, tiled=True)  58.3 us
    dot_general x2, matrix products, multiply(): jnp.dot(lax.all_gather(left, 'col', axis=1, tiled=True), right_all, prefe...  16.5 us
  transfers between devices with their start and end apart: 4, of which 4 were waited for; matrix products, arithmetic and copies ran while one was open for 4% of the time, Pallas kernels for 0%

commit v1 on v0

--- a/solution.py
+++ b/solution.py
@@ -2,6 +2,7 @@
 import jax.numpy as jnp
 from jax import lax
 from jax.sharding import PartitionSpec as P
+from jax.lax import all_to_all, axis_size
 
 
 def split_up(array, dim, size):
@@ -27,11 +28,11 @@
         groups * width, columns
     )
     right_all = lax.all_gather(own_rows, "row", axis=0, tiled=True)
-    return jnp.dot(
-        lax.all_gather(left, "col", axis=1, tiled=True),
-        right_all,
-        preferred_element_type=jnp.float32,
+    _hold_turns = lambda here_x, mesh_dim, out_dim: jnp.concatenate(
+        all_to_all(jnp.stack([here_x for _ in range(axis_size(mesh_dim))], axis=0), mesh_dim, 0, 0),
+        out_dim,
     )
+    return jnp.dot(_hold_turns(left, "col", 1), right_all, preferred_element_type=jnp.float32)
 
 
 def per_device(left, middle, right):

time: 291 us -> 363 us (1.25)
  local copies, waits for them, and re-layouts: 5.97 us -> 36.6 us
  waiting for transfers between devices: 194 us -> 223 us
  starting transfers between devices: 0.12 us -> 14.1 us
    all_to_all x0 -> x2, waiting for transfers between devices: none -> 165 us  [multiply(): all_to_all(jnp.stack([here_x for _ in range(axis_size(mesh_dim))], axis=0...]
    all_gather x2 -> x0, waiting for transfers between devices: 120 us -> none  [multiply(): lax.all_gather(left, 'col', axis=1, tiled=True)]
    reshape x0 -> x3, local copies, waits for them, and re-layouts: none -> 25.9 us  [the longest x2 24.9 us: multiply(): jnp.concatenate(all_to_all(jnp.stack([here_x for _ in range(axis_size(mes...]
    all_gather x2, waiting for transfers between devices: 73.8 us -> 58 us  [multiply(): right_all = lax.all_gather(own_rows, 'row', axis=0, tiled=True)]
    all_to_all x0 -> x2, starting transfers between devices: none -> 14 us  [multiply(): all_to_all(jnp.stack([here_x for _ in range(axis_size(mesh_dim))], axis=0...]
    another operation x0 -> x2, local copies, waits for them, and re-layouts: none -> 8.33 us  [multiply(): jnp.stack([here_x for _ in range(axis_size(mesh_dim))], axis=0)]
  transfers between devices with their start and end apart: 4 -> 4, of which waited for: 4 -> 3; matrix products, arithmetic and copies ran while one was open for 4% -> 7% of each run, Pallas kernels for 0% -> 0%
where the time goes in v1:
time: 363 us; the launch traced here: 361 us
  waiting for transfers between devices  223 us (61%)
  blocking collectives  56.9 us (16%)
  local copies, waits for them, and re-layouts  36.6 us (10%)
  matrix products  16.5 us (5%)
  starting transfers between devices  14.1 us (4%)
  between operations  13.5 us (4%)
    all_to_all x2, waiting for transfers between devices, multiply(): all_to_all(jnp.stack([here_x for _ in range(axis_size(mesh_dim))], axis=0...  165 us
    all_gather x2, waiting for transfers between devices, multiply(): right_all = lax.all_gather(own_rows, 'row', axis=0, tiled=True)  58 us
    all_to_all x2, blocking collectives, sum_at_owner(): lax.all_to_all(blocks, axis, split_axis=0, concat_axis=0, tiled=True)  56.9 us
    reshape x2, local copies, waits for them, and re-layouts, multiply(): jnp.concatenate(all_to_all(jnp.stack([here_x for _ in range(axis_size(mes...  24.9 us
    dot_general x2, matrix products, multiply(): jnp.dot(_hold_turns(left, 'col', 1), right_all, preferred_element_type=jn...  16.5 us
    all_to_all x2, starting transfers between devices, multiply(): all_to_all(jnp.stack([here_x for _ in range(axis_size(mesh_dim))], axis=0...  14 us
    another operation x2, local copies, waits for them, and re-layouts, multiply(): jnp.stack([here_x for _ in range(axis_size(mesh_dim))], axis=0)  8.33 us
  transfers between devices with their start and end apart: 4, of which 3 were waited for; matrix products, arithmetic and copies ran while one was open for 7% of the time, Pallas kernels for 0%

profile of v1, /device:TPU:1, one launch (start us, length us, event | category | flops | bytes accessed | tf_op | source)
XLA Modules:
  0.0 361.3 jit_solution(17670917914619328528)
XLA Ops:
  6.5 0.0 copy-start
  6.5 1.3 copy.7
  7.9 4.3 %stack.4 = bf16[16,1024,256]{1,2,0:T(8,128)(2,1)} broadcast(bf16[1024,256]{0,1:T(8,128)(2,1)S(1)} %copy.7), dimensions={1,2} | broadcast | bytes 8912896 | tf_op jit(solution)/shard_map/stack | solution.py:32
  12.2 7.7 %all-to-all-start = ((bf16[16,1024,256]{1,2,0:T(8,128)(2,1)}), bf16[16,1024,256]{1,2,0:T(8,128)(2,1)}, u32[]{:S(2)}, u32[]{:S(2)}) async-start(bf16[16,1024,256]{1,2,0:T(8,128)(2,1)} %stack.4), calls=%async_computation | async-start | bytes 16777216 | tf_op jit(solution)/shard_map/all_to_all | solution.py:32
  19.8 0.0 all-gather.3.cloned.1.call-start
  19.9 0.8 constant_dynamic-slice_fusion.1
  20.7 0.0 all-gather.3.cloned.1.call-update
  20.8 58.0 %all-gather.3.cloned.1.call-done = bf16[4096,512]{1,0:T(8,128)(2,1)} async-done(((bf16[512,512]{1,0:T(8,128)(2,1)}), bf16[4096,512]{1,0:T(8,128)(2,1)}) %all-gather.3.cloned.1.call-update) | async-done | bytes 4194320 | tf_op jit(solution)/shard_map/all_gather | solution.py:30
  78.7 53.4 %all-to-all-done = bf16[16,1024,256]{1,2,0:T(8,128)(2,1)} async-done(((bf16[16,1024,256]{1,2,0:T(8,128)(2,1)}), bf16[16,1024,256]{1,2,0:T(8,128)(2,1)}, u32[]{:S(2)}, u32[]{:S(2)}) %all-to-all-start) | async-done | bytes 8388640 | tf_op jit(solution)/shard_map/all_to_all | solution.py:32
  132.1 8.2 %fusion = f32[512,1024]{1,0:T(8,128)S(1)} fusion(bf16[4096,512]{1,0:T(8,128)(2,1)} %all-gather.3.cloned.1.call-done, bf16[1024,4096]{0,1:T(8,128)(2,1)} %bitcast.3), kind=kOutput, calls=%fused_computation.3 | convolution fusion | flops 4294967296 | bytes 14680064 | tf_op jit(solution)/shard_map/dot_general | solution.py:35
  140.4 28.6 %all_to_all.20 = f32[2,1024,256]{1,2,0:T(8,128)S(1)} all-to-all(f32[2,1024,256]{1,2,0:T(8,128)S(1)} %bitcast.23), channel_id=1, replica_groups=mesh['row'=8,'col'=16,'layer'=2] {'layer'}, dimensions={0} | all-to-all | bytes 4194304 | tf_op jit(solution)/shard_map/all_to_all | solution.py:16
  168.9 0.2 reduce_sum.18
  169.1 0.2 copy.8
  169.3 4.0 %stack.5 = bf16[16,1024,256]{2,1,0:T(8,128)(2,1)} broadcast(bf16[1024,256]{1,0:T(8,128)(2,1)S(1)} %copy.8), dimensions={1,2} | broadcast | bytes 8912896 | tf_op jit(solution)/shard_map/stack | solution.py:32
  173.4 6.3 %all-to-all-start.2 = ((bf16[16,1024,256]{2,1,0:T(8,128)(2,1)}), bf16[16,1024,256]{2,1,0:T(8,128)(2,1)}, u32[]{:S(2)}, u32[]{:S(2)}) async-start(bf16[16,1024,256]{2,1,0:T(8,128)(2,1)} %stack.5), calls=%async_computation.2 | async-start | bytes 16777216 | tf_op jit(solution)/shard_map/all_to_all | solution.py:32
  179.7 0.0 all-gather.5.cloned.1.call-start
  179.8 1.0 copy.11
  180.8 0.0 all-gather.5.cloned.1.call-update
  180.8 111.1 %all-to-all-done.2 = bf16[16,1024,256]{2,1,0:T(8,128)(2,1)} async-done(((bf16[16,1024,256]{2,1,0:T(8,128)(2,1)}), bf16[16,1024,256]{2,1,0:T(8,128)(2,1)}, u32[]{:S(2)}, u32[]{:S(2)}) %all-to-all-start.2) | async-done | bytes 8388640 | tf_op jit(solution)/shard_map/all_to_all | solution.py:32
  292.0 11.4 %copy.9 = bf16[1024,16,256]{2,1,0:T(8,128)(2,1)} copy(bf16[1024,16,256]{2,0,1:T(8,128)(2,1)} %bitcast.7) | data formatting | bytes 16777216 | tf_op jit(solution)/shard_map/reshape | solution.py:31
  303.4 13.5 %reshape.44 = bf16[1024,4096,1]{1,0,2:T(8,128)(2,1)} reshape(bf16[1024,16,256]{2,1,0:T(8,128)(2,1)} %copy.9) | data formatting | bytes 16777216 | tf_op jit(solution)/shard_map/reshape | solution.py:31
  316.9 8.3 %convolution_bitcast_fusion = f32[2,1024,256]{2,1,0:T(8,128)S(1)} fusion(bf16[1024,4096,1]{1,0,2:T(8,128)(2,1)} %reshape.44, bf16[2,256,4096]{2,1,0:T(8,128)(2,1)} %bitcast.27), kind=kOutput, calls=%fused_computation | convolution fusion | flops 4294967296 | bytes 14680064 | tf_op jit(solution)/shard_map/dot_general | solution.py:35
  325.1 28.3 %all_to_all.21 = f32[2,1024,256]{2,1,0:T(8,128)S(1)} all-to-all(f32[2,1024,256]{2,1,0:T(8,128)S(1)} %convolution_bitcast_fusion), channel_id=1, replica_groups=mesh['row'=8,'col'=16,'layer'=2] {'layer'}, dimensions={0} | all-to-all | bytes 4194304 | tf_op jit(solution)/shard_map/all_to_all | solution.py:16
  353.4 1.1 reduce_sum.19
  (7 shorter events, 0.1 us)
Async XLA Ops:
  6.5 13.4 %copy-start = (bf16[1024,512]{1,0:T(8,128)(2,1)S(1)}, bf16[1024,512]{1,0:T(8,128)(2,1)}, u32[]{:S(2)}) copy-start(bf16[1024,512]{1,0:T(8,128)(2,1)} %param.4) | copy-start | bytes 3145732
  12.2 120.0 %all-to-all-start = ((bf16[16,1024,256]{1,2,0:T(8,128)(2,1)}), bf16[16,1024,256]{1,2,0:T(8,128)(2,1)}, u32[]{:S(2)}, u32[]{:S(2)}) async-start(bf16[16,1024,256]{1,2,0:T(8,128)(2,1)} %stack.4), calls=%async_computation | async-start | bytes 16777216 | tf_op jit(solution)/shard_map/all_to_all | solution.py:32
  19.8 58.9 %all-gather.3.cloned.1.call-start = ((), (), s32[]{:S(2)}) async-start(), calls=%async_computation.4 | async-start | bytes 4718592 | tf_op jit(solution)/shard_map/all_gather | solution.py:30
  173.4 6.4 %copy-start.2 = (bf16[1024,512]{1,0:T(8,128)(2,1)S(1)}, bf16[1024,512]{1,0:T(8,128)(2,1)}, u32[]{:S(2)}) copy-start(bf16[1024,512]{1,0:T(8,128)(2,1)} %param.5) | copy-start | bytes 3145732
  173.4 118.6 %all-to-all-start.2 = ((bf16[16,1024,256]{2,1,0:T(8,128)(2,1)}), bf16[16,1024,256]{2,1,0:T(8,128)(2,1)}, u32[]{:S(2)}, u32[]{:S(2)}) async-start(bf16[16,1024,256]{2,1,0:T(8,128)(2,1)} %stack.5), calls=%async_computation.2 | async-start | bytes 16777216 | tf_op jit(solution)/shard_map/all_to_all | solution.py:32
  179.7 137.1 %all-gather.5.cloned.1.call-start = ((), (), s32[]{:S(2)}) async-start(), calls=%async_computation.5 | async-start | bytes 4718592 | tf_op jit(solution)/shard_map/all_gather | solution.py:30
  316.8 37.7 %copy-start.1 = (bf16[1024,512]{1,0:T(8,128)(2,1)S(1)}, bf16[1024,512]{1,0:T(8,128)(2,1)}, u32[]{:S(2)}) copy-start(bf16[1024,512]{1,0:T(8,128)(2,1)} %param.4) | copy-start | bytes 3145732
Sparse Core Ops, SparseCore 0:
  22.4 56.2 all-gather.2
  182.3 55.7 all-gather.4
